TPU v7x, 512 devices: a whole 4x8x8 slice. The times are simulated.
512 devices in a mesh: row: 16 (over x, y_lo, core), col: 32 (over z, y_hi).
Axes of the slice: x: 4, y: 8 (y_hi: 4, y_lo: 2; y = y_hi * 2 + y_lo), z: 8, core: 2. Of those that a mesh axis runs over, the one named last changes fastest.
Arguments:
- item_ids: int32 [131072], P(('row', 'col')), may hold values from 0 to 1023
- user_lengths: int32 [32], replicated, may hold values from 1 to 8192, 131072 in all
- catalogue: bfloat16 [1024, 1024], P(('row', 'col')), may hold values from -6 to 6
- tap_lengths: int32 [1, 1024], replicated, may hold values from 64 to 256
- conv_taps: bfloat16 [1, 256, 1024], replicated, may hold values from -0.375 to 0.375
- norm_gains: float32 [1, 2, 1024], replicated, may hold values from 0.1 to 1.9
- gate_weight: bfloat16 [1, 1024, 1024], P(None, 'col'), may hold values from -0.1875 to 0.1875
- up_weight: bfloat16 [1, 1024, 1024], P(None, 'col'), may hold values from -0.1875 to 0.1875
- down_weight: bfloat16 [1, 1024, 1024], P(None, 'col'), may hold values from -0.1875 to 0.1875
Outputs:
- history_out: bfloat16 [131072, 1024], P(('row', 'col'))
Inputs may be any that keep to these rules, and one draw needn't show every extreme that they name: `user_lengths`: the 32 lengths sum to 131072.
All inputs are finite; a program needn't handle non-finite values.
Results may differ from a plain program's by a relative error of at most 0.0054.
Values may be sent and summed in bfloat16 or wider, within the bound.
A program may use at most 64 MiB of HBM per device.

v0:
```python
import jax
import jax.numpy as jnp
from jax import lax
from jax.sharding import Mesh
from jax.sharding import PartitionSpec as P

ROW_COL = ("row", "col_0", "col_1")
COL = ("col_0", "col_1")
epsilon = 1e-06
group_taps = 32


def from_behind(block, axis, distance):
    devices = range(lax.axis_size(axis))
    route = [(i - distance, i) for i in devices if i - distance in devices]
    return lax.ppermute(block, axis, route)


def in_one_piece(arrays, axis, dim, along):
    both = jnp.concatenate(arrays, axis=along)
    result, at, outs = (lax.all_gather(both, axis, axis=dim, tiled=True), 0, [])
    for a in arrays:
        outs.append(lax.slice_in_dim(result, at, at + a.shape[along], axis=along))
        at += a.shape[along]
    return tuple(outs)


def whole_of(array, axes, dim):
    result = array
    for number in range(len(axes) - 1, -1, -1):
        result = lax.all_gather(result, axes[number], axis=dim, tiled=True)
    return result


def rms_norm(values, gains):
    scale = lax.rsqrt(jnp.mean(values * values, axis=-1, keepdims=True) + epsilon)
    return values * scale * gains


def token_ages(positions, user_starts):
    reached = user_starts[None, :] <= positions[:, None]
    fallback = jnp.minimum(positions, 0)[:, None]
    seg_start = jnp.max(jnp.where(reached, user_starts[None, :], fallback), axis=1)
    return positions - seg_start


def earlier_items(item_ids, wanted):
    current = item_ids
    pieces = []
    current = from_behind(current, ROW_COL, 1)
    pieces = [current] + pieces
    return pieces[0][-wanted:]


def convolve(extended, tap_table, token_age, out_rows):
    reach = extended.shape[0] - out_rows
    groups = -(-tap_table.shape[0] // group_taps)

    def one_group(group_index, accumulated):
        for within in range(group_taps):
            lag_index = group_index * group_taps + within
            shifted = lax.dynamic_slice_in_dim(extended, reach - lag_index, out_rows, 0)
            weights = lax.dynamic_slice_in_dim(tap_table, lag_index, 1, 0)
            keep = (lag_index <= token_age)[:, None]
            accumulated = accumulated + jnp.where(keep, shifted * weights, 0.0)
        return accumulated

    blank = jnp.zeros((out_rows, extended.shape[1]), jnp.float32)
    return lax.fori_loop(0, groups, one_group, blank)


def feed_forward(hidden, gains_row, gate_rows, up_rows, down_rows):
    inner = rms_norm(hidden, gains_row).astype(jnp.bfloat16)
    shards = in_one_piece((gate_rows, up_rows), COL, 0, 1)
    columns = inner
    first_sum = jnp.dot(columns, shards[0], preferred_element_type=jnp.float32)
    second_sum = jnp.dot(columns, shards[1], preferred_element_type=jnp.float32)
    activated = (jax.nn.silu(first_sum) * second_sum).astype(jnp.bfloat16)
    columns = activated
    projected = jnp.dot(columns, whole_of(down_rows, COL, 0), preferred_element_type=jnp.float32)
    return hidden + projected


def body(
    item_ids,
    user_lengths,
    catalogue,
    tap_lengths,
    conv_taps,
    norm_gains,
    gate_weight,
    up_weight,
    down_weight,
):
    row_count = item_ids.shape[0]
    reach = conv_taps.shape[1] - 1
    layer_count = conv_taps.shape[0]
    catalogue_all = lax.all_gather(catalogue, ROW_COL, axis=0, tiled=True)
    device_index = lax.axis_index("row") * lax.axis_size(COL) + lax.axis_index(COL)
    first_row = device_index * row_count
    user_starts = jnp.cumsum(user_lengths) - user_lengths
    lag_column = jnp.arange(conv_taps.shape[1], dtype=jnp.int32)[:, None]
    tap_tables = conv_taps.astype(jnp.float32) * (
        lag_column[None] < tap_lengths[:, None, :]
    ).astype(jnp.float32)
    extra = reach * layer_count
    wide_ids = jnp.concatenate([earlier_items(item_ids, extra), item_ids], axis=0)
    hidden = jnp.take(catalogue_all, wide_ids, axis=0).astype(jnp.float32)
    positions = first_row - extra + jnp.arange(row_count + extra, dtype=jnp.int32)
    all_ages = token_ages(positions, user_starts)
    out_rows = row_count + reach * (layer_count - 1)
    normed = rms_norm(hidden, norm_gains[0, 0]).astype(jnp.bfloat16)
    hidden = hidden[-out_rows:] + convolve(normed, tap_tables[0], all_ages[-out_rows:], out_rows)
    hidden = feed_forward(hidden, norm_gains[0, 1], gate_weight[0], up_weight[0], down_weight[0])
    return hidden.astype(jnp.bfloat16)


def solution(mesh):
    finer = Mesh(mesh.devices.reshape(mesh.shape["row"], 8, 4), ("row", "col_0", "col_1"))
    placed = (
        P(ROW_COL),
        P(),
        P(ROW_COL, None),
        P(),
        P(),
        P(),
        P(None, COL, None),
        P(None, COL, None),
        P(None, COL, None),
    )
    return jax.shard_map(
        body, mesh=finer, in_specs=placed, out_specs=P(ROW_COL, None), check_vma=False
    )
```

profile of v0, /device:TPU:2, one launch (start us, length us, event | category | flops | bytes accessed | tf_op | source)
XLA Modules:
  0.0 1239.3 jit_solution(7251413055012605955)
XLA Ops:
  6.5 0.0 all-gather.11.cloned.1.call-start
  6.5 0.7 all-gather.11.cloned.1.call-update
  7.3 0.0 all-gather.7.cloned.1.call-start
  7.3 1.5 pad_maximum_fusion
  8.8 0.0 all-gather.7.cloned.1.call-update
  8.9 0.0 all-gather.9.cloned.1.call-start
  8.9 4.5 collective-permute-start
  13.4 16.6 %all-gather = bf16[1,128,1024]{2,1,0:T(8,128)(2,1)} all-gather(bf16[1,32,1024]{2,1,0:T(8,128)(2,1)} %param.19), channel_id=2, replica_groups=mesh['row'=16,'col_0'=8,'col_1'=4] {'col_1'}, dimensions={1}, use_global_device_ids=true | all-gather | bytes 327680 | tf_op jit(solution)/shard_map/all_gather | solution.py:31
  30.0 0.0 all-gather.9.cloned.1.call-update
  30.1 0.7 copy.13
  30.8 0.1 reduce-window.9
  30.9 0.1 reduce
  31.0 0.7 sub.362
  31.6 0.8 fusion.52
  32.4 2.2 select_bitcast_fusion
  34.7 0.1 select_reduce_fusion
  34.8 0.1 slice.23
  34.9 0.0 collective-permute-done
  34.9 0.1 slice.21
  34.9 0.0 copy-done.3
  34.9 0.1 compare_and_fusion
  35.0 0.1 compare_select_fusion
  35.1 1044.8 %all-gather.11.cloned.1.call-done = bf16[512,2,1024]{2,1,0:T(2,128)(2,1)} async-done(((bf16[1,2,1024]{2,1,0:T(2,128)(2,1)}), bf16[512,2,1024]{2,1,0:T(2,128)(2,1)}) %all-gather.11.cloned.1.call-update) | async-done | bytes 2097168 | tf_op jit(solution)/shard_map/all_gather | solution.py:98
  1079.9 2.7 reshape.388
  1082.6 2.8 gather_fusion
  1085.4 1.7 multiply_reduce_fusion
  1087.1 1.6 multiply_convert_fusion
  1088.7 0.0 copy-start
  1088.7 125.7 %while.17 = (s32[]{:T(128)}, f32[256,1024]{1,0:T(8,128)S(1)}, s32[256]{0:T(256)S(1)}, bf16[511,1024]{1,0:T(8,128)(2,1)S(1)}, f32[256,1024]{1,0:T(8,128)}, /*inde...) while((s32[]{:T(128)}, f32[256,1024]{1,0:T(8,128)S(1)}, ...), condition=%wide.region_4.5_spmd.clone, body=%wide.region_3.4_spmd.clone.sunk | while | flops 33825024 | bytes 19289948 | solution.py:69
  1088.8 1.3 constant_dynamic-slice_fusion.35
  1090.2 1.4 constant_dynamic-slice_fusion.34
  1092.0 12.2 select_add_fusion.3
  1104.3 1.4 constant_dynamic-slice_fusion.35
  1105.9 1.5 constant_dynamic-slice_fusion.34
  1107.7 12.2 select_add_fusion.3
  1120.0 1.5 constant_dynamic-slice_fusion.35
  1121.6 1.4 constant_dynamic-slice_fusion.34
  1123.4 12.2 select_add_fusion.3
  1135.7 1.5 constant_dynamic-slice_fusion.35
  1137.3 1.4 constant_dynamic-slice_fusion.34
  1139.1 12.2 select_add_fusion.3
  1151.4 1.4 constant_dynamic-slice_fusion.35
  1152.9 1.7 constant_dynamic-slice_fusion.34
  1155.0 12.2 select_add_fusion.3
  1167.3 1.4 constant_dynamic-slice_fusion.35
  1168.8 1.7 constant_dynamic-slice_fusion.34
  1170.9 12.2 select_add_fusion.3
  1183.2 1.3 constant_dynamic-slice_fusion.35
  1184.6 1.7 constant_dynamic-slice_fusion.34
  1186.7 12.2 select_add_fusion.3
  1199.0 1.3 constant_dynamic-slice_fusion.35
  1200.4 1.4 constant_dynamic-slice_fusion.34
  1202.2 12.2 select_add_fusion.3
  1214.4 0.0 copy-done
  1214.4 0.2 fusion.51
  1214.6 0.0 copy-start.1
  1214.6 1.3 copy-done.1
  1216.0 0.3 multiply_reduce_fusion.1
  1216.2 0.0 all-gather.7.cloned.1.call-done
  1216.3 0.0 copy-start.2
  1216.3 3.9 fusion.26
  1220.2 7.7 all-gather.9.cloned.1.call-done
  1228.0 0.0 copy-done.2
  1228.0 4.8 fusion.39
  (23 shorter events, 0.6 us)
Async XLA Ops:
  6.5 28.4 %copy-start.3 = (s32[256]{0:T(256)S(1)}, s32[256]{0:T(256)}, u32[]{:S(2)}) copy-start(s32[256]{0:T(256)} %param.11) | copy-start | bytes 3076
  6.5 1073.3 %all-gather.11.cloned.1.call-start = ((), (), s32[]{:S(2)}) async-start(), calls=%async_computation.2 | async-start | bytes 2101248 | tf_op jit(solution)/shard_map/all_gather | solution.py:98
  7.3 1209.0 %all-gather.7.cloned.1.call-start = ((), (), s32[]{:S(2)}) async-start(), calls=%async_computation | async-start | bytes 4325376 | tf_op jit(solution)/shard_map/all_gather | solution.py:21
  8.9 1219.1 %all-gather.9.cloned.1.call-start = ((), (), s32[]{:S(2)}) async-start(), calls=%async_computation.1 | async-start | bytes 2359296 | tf_op jit(solution)/shard_map/all_gather | solution.py:31
  8.9 25.9 %collective-permute-start = (s32[256]{0:T(256)}, s32[256]{0:T(256)S(1)}, u32[]{:S(2)}, u32[]{:S(2)}) collective-permute-start(s32[256]{0:T(256)} %param.11), channel_id=1, source_target_pairs={{0,1},{1,2},{2,3},{3,4},{4,5},{5,6},{6,7},{7,8},{8,9},{9,10},{10,1... | collective-permute-start | bytes 3080 | tf_op jit(solution)/shard_map/ppermute | solution.py:16
  1088.7 125.7 %copy-start = (bf16[511,1024]{1,0:T(8,128)(2,1)S(1)}, bf16[511,1024]{1,0:T(8,128)(2,1)}, u32[]{:S(2)}) copy-start(bf16[511,1024]{1,0:T(8,128)(2,1)} %gather_fusion) | copy-start | bytes 3139588
  1214.6 1.3 copy-start.1
  1216.3 11.7 copy-start.2
Sparse Core Ops, SparseCore 0:
  9.5 1070.3 all-gather.10
  1083.0 103.2 all-gather.6
  1188.4 39.5 all-gather.8
where the time goes:
time: 1240 us
  waiting for transfers between devices  1050 us (85%)
  other arithmetic  107 us (9%)
  local copies, waits for them, and re-layouts  31.9 us (3%)
  blocking collectives  16.6 us (1%)
  between operations  13.2 us (1%)
    all_gather x1, waiting for transfers between devices, body(): catalogue_all = lax.all_gather(catalogue, ROW_COL, axis=0, tiled=True)  1040 us
    add x8, other arithmetic, one_group(): accumulated = accumulated + jnp.where(keep, shifted * weights, 0.0)  97.5 us
  transfers between devices with their start and end apart: 4, of which 2 were waited for; matrix products, arithmetic and copies ran while one was open for 11% of the time, Pallas kernels for 0%

commit v1 on v0

--- a/solution.py
+++ b/solution.py
@@ -95,7 +95,12 @@
     row_count = item_ids.shape[0]
     reach = conv_taps.shape[1] - 1
     layer_count = conv_taps.shape[0]
-    catalogue_all = lax.all_gather(catalogue, ROW_COL, axis=0, tiled=True)
+    catalogue_all = jnp.concatenate(
+        lax.all_to_all(
+            jnp.stack(tuple((catalogue for _ in range(lax.axis_size(ROW_COL)))), 0), ROW_COL, 0, 0
+        ),
+        0,
+    )
     device_index = lax.axis_index("row") * lax.axis_size(COL) + lax.axis_index(COL)
     first_row = device_index * row_count
     user_starts = jnp.cumsum(user_lengths) - user_lengths

time: 1240 us -> 248 us (0.20)
  the two profiles are of different devices: /device:TPU:2 before, /device:TPU:16 now
where the time goes in v1:
time: 248 us; the launch traced here: 246 us
  other arithmetic  105 us (42%)
  blocking collectives  52.1 us (21%)
  local copies, waits for them, and re-layouts  33.6 us (14%)
  starting transfers between devices  28.7 us (12%)
  between operations  13.6 us (5%)
  matrix products  8.71 us (4%)
  loops' own time  4.23 us (2%)
    add x8, other arithmetic, one_group(): accumulated = accumulated + jnp.where(keep, shifted * weights, 0.0)  97.5 us
    all_gather x1, blocking collectives, whole_of(): result = lax.all_gather(result, axes[number], axis=dim, tiled=True)  52.1 us
    dynamic_slice x16, local copies, waits for them, and re-layouts, one_group(): weights = lax.dynamic_slice_in_dim(tap_table, lag_index, 1, 0)  23.3 us
    all_to_all x1, starting transfers between devices, body(): lax.all_to_all(jnp.stack(tuple((catalogue for _ in range(lax.axis_size(RO...  23.1 us
    ppermute x1, starting transfers between devices, from_behind(): return lax.ppermute(block, axis, route)  5.59 us
  transfers between devices with their start and end apart: 4, of which 0 were waited for; matrix products, arithmetic and copies ran while one was open for 57% of the time, Pallas kernels for 0%

profile of v1, /device:TPU:16, one launch (start us, length us, event | category | flops | bytes accessed | tf_op | source)
XLA Modules:
  0.0 246.0 jit_solution(17726425656835040291)
XLA Ops:
  6.5 0.0 all-gather.5.cloned.1.call-start
  6.5 1.5 pad_maximum_fusion
  8.1 0.0 all-gather.5.cloned.1.call-update
  8.1 3.1 %stack.2 = bf16[512,2,1024]{2,1,0:T(2,128)(2,1)} broadcast(bf16[2,1024]{1,0:T(2,128)(2,1)} %param.13), dimensions={1,2} | broadcast | bytes 2101248 | tf_op jit(solution)/shard_map/stack | solution.py:100
  11.2 0.0 copy-start.3
  11.2 0.0 copy-start.6
  11.3 23.1 %all-to-all-start = ((bf16[512,2,1024]{2,1,0:T(2,128)(2,1)}), bf16[512,2,1024]{2,1,0:T(2,128)(2,1)}, u32[]{:S(2)}, u32[]{:S(2)}) async-start(bf16[512,2,1024]{2,1,0:T(2,128)(2,1)} %stack.2), calls=%async_computation | async-start | bytes 4194304 | tf_op jit(solution)/shard_map/all_to_all | solution.py:99
  34.4 0.0 all-gather.7.cloned.1.call-start
  34.4 0.0 copy-done.7
  34.4 5.6 %collective-permute-start = (s32[256]{0:T(256)S(1)}, s32[256]{0:T(256)S(1)}, u32[]{:S(2)}, u32[]{:S(2)}) collective-permute-start(s32[256]{0:T(256)S(1)} %copy-done.7), channel_id=1, source_target_pairs={{0,1},{1,2},{2,3},{3,4},{4,5},{5,6},{6,7},{7,8},{8,9},{9,10},{10,1... | collective-permute-start | bytes 3080 | tf_op jit(solution)/shard_map/ppermute | solution.py:16
  40.0 0.0 copy-done.4
  40.0 52.1 %all-gather = bf16[1,128,1024]{2,1,0:T(8,128)(2,1)} all-gather(bf16[1,32,1024]{2,1,0:T(8,128)(2,1)S(1)} %copy-done.4), channel_id=2, replica_groups=mesh['row'=16,'col_0'=8,'col_1'=4] {'col_1'}, dimensions={1}, use_global_device_ids=true | all-gather | bytes 327680 | tf_op jit(solution)/shard_map/all_gather | solution.py:31
  92.2 0.0 all-gather.7.cloned.1.call-update
  92.2 0.0 copy-done.8
  92.2 0.1 copy.12
  92.3 0.1 reduce-window.9
  92.4 0.1 reduce
  92.5 0.1 select_reduce_fusion
  92.6 0.0 copy-done.5
  92.6 0.0 copy-done.3
  92.6 0.0 copy-done.6
  92.6 1.1 select_bitcast_fusion
  93.8 0.1 slice.23
  93.9 0.0 collective-permute-done
  93.9 0.1 slice.21
  93.9 0.1 compare_and_fusion
  94.0 0.1 compare_select_fusion
  94.1 0.0 all-to-all-done
  94.1 2.8 %reshape.380 = bf16[1024,1024]{1,0:T(8,128)(2,1)S(1)} reshape(bf16[512,2,1024]{2,1,0:T(2,128)(2,1)} %all-to-all-done) | data formatting | bytes 4194304 | tf_op jit(solution)/shard_map/reshape | solution.py:98
  96.9 2.8 %gather_fusion = bf16[511,1024]{1,0:T(8,128)(2,1)} fusion(bf16[1024,1024]{1,0:T(8,128)(2,1)S(1)} %reshape.380, s32[1024]{0:T(1024)S(1)} %pad_clamp_fusion), kind=kCustom, calls=%fused_computation | custom fusion | bytes 2095100 | tf_op jit(solution)/shard_map/jit(_take)/gather | solution.py:113
  99.7 1.7 multiply_reduce_fusion
  101.3 1.6 multiply_convert_fusion
  103.0 125.6 %while.17 = (s32[]{:T(128)}, f32[256,1024]{1,0:T(8,128)S(1)}, s32[256]{0:T(256)S(1)}, bf16[511,1024]{1,0:T(8,128)(2,1)S(1)}, f32[256,1024]{1,0:T(8,128)}, /*inde...) while((s32[]{:T(128)}, f32[256,1024]{1,0:T(8,128)S(1)}, ...), condition=%wide.region_4.5_spmd.clone, body=%wide.region_3.4_spmd.clone.sunk | while | flops 33825024 | bytes 19289948 | solution.py:69
  103.1 1.5 constant_dynamic-slice_fusion.35
  104.7 1.6 constant_dynamic-slice_fusion.34
  106.7 12.2 %select_add_fusion.3 = f32[256,1024]{1,0:T(8,128)S(1)} fusion(f32[256,1024]{1,0:T(8,128)S(1)} %get-tuple-element.605, f32[1024]{0:T(1024)S(1)} %bitcast.115, bf16[511,1024]{1,0:T(8,128)(2,1)S(1)} %get-tuple-element.679, s32[]{:T(128)S(6)} %select_n.1373, f32[1024]{0:T(1024)S(1)} %bitcast.116, s32[]{:T(128)S(6)} %select_n.1374, ...), kind=kLoop, calls=%fused_computation.26.clone.1 | loop fusion | flops 33816576 | bytes 19013760 | tf_op jit(solution)/shard_map/while/body/eval_jaxpr/add | solution.py:65
  119.0 1.5 constant_dynamic-slice_fusion.35
  120.6 1.5 constant_dynamic-slice_fusion.34
  122.4 12.2 %select_add_fusion.3 = f32[256,1024]{1,0:T(8,128)S(1)} fusion(f32[256,1024]{1,0:T(8,128)S(1)} %get-tuple-element.605, f32[1024]{0:T(1024)S(1)} %bitcast.115, bf16[511,1024]{1,0:T(8,128)(2,1)S(1)} %get-tuple-element.679, s32[]{:T(128)S(6)} %select_n.1373, f32[1024]{0:T(1024)S(1)} %bitcast.116, s32[]{:T(128)S(6)} %select_n.1374, ...), kind=kLoop, calls=%fused_computation.26.clone.1 | loop fusion | flops 33816576 | bytes 19013760 | tf_op jit(solution)/shard_map/while/body/eval_jaxpr/add | solution.py:65
  134.7 1.5 constant_dynamic-slice_fusion.35
  136.3 1.5 constant_dynamic-slice_fusion.34
  138.1 12.2 %select_add_fusion.3 = f32[256,1024]{1,0:T(8,128)S(1)} fusion(f32[256,1024]{1,0:T(8,128)S(1)} %get-tuple-element.605, f32[1024]{0:T(1024)S(1)} %bitcast.115, bf16[511,1024]{1,0:T(8,128)(2,1)S(1)} %get-tuple-element.679, s32[]{:T(128)S(6)} %select_n.1373, f32[1024]{0:T(1024)S(1)} %bitcast.116, s32[]{:T(128)S(6)} %select_n.1374, ...), kind=kLoop, calls=%fused_computation.26.clone.1 | loop fusion | flops 33816576 | bytes 19013760 | tf_op jit(solution)/shard_map/while/body/eval_jaxpr/add | solution.py:65
  150.4 1.5 constant_dynamic-slice_fusion.35
  152.0 1.4 constant_dynamic-slice_fusion.34
  153.8 12.2 %select_add_fusion.3 = f32[256,1024]{1,0:T(8,128)S(1)} fusion(f32[256,1024]{1,0:T(8,128)S(1)} %get-tuple-element.605, f32[1024]{0:T(1024)S(1)} %bitcast.115, bf16[511,1024]{1,0:T(8,128)(2,1)S(1)} %get-tuple-element.679, s32[]{:T(128)S(6)} %select_n.1373, f32[1024]{0:T(1024)S(1)} %bitcast.116, s32[]{:T(128)S(6)} %select_n.1374, ...), kind=kLoop, calls=%fused_computation.26.clone.1 | loop fusion | flops 33816576 | bytes 19013760 | tf_op jit(solution)/shard_map/while/body/eval_jaxpr/add | solution.py:65
  166.1 1.3 constant_dynamic-slice_fusion.35
  167.5 1.6 constant_dynamic-slice_fusion.34
  169.5 12.2 %select_add_fusion.3 = f32[256,1024]{1,0:T(8,128)S(1)} fusion(f32[256,1024]{1,0:T(8,128)S(1)} %get-tuple-element.605, f32[1024]{0:T(1024)S(1)} %bitcast.115, bf16[511,1024]{1,0:T(8,128)(2,1)S(1)} %get-tuple-element.679, s32[]{:T(128)S(6)} %select_n.1373, f32[1024]{0:T(1024)S(1)} %bitcast.116, s32[]{:T(128)S(6)} %select_n.1374, ...), kind=kLoop, calls=%fused_computation.26.clone.1 | loop fusion | flops 33816576 | bytes 19013760 | tf_op jit(solution)/shard_map/while/body/eval_jaxpr/add | solution.py:65
  181.8 1.2 constant_dynamic-slice_fusion.35
  183.1 1.5 constant_dynamic-slice_fusion.34
  185.0 12.2 %select_add_fusion.3 = f32[256,1024]{1,0:T(8,128)S(1)} fusion(f32[256,1024]{1,0:T(8,128)S(1)} %get-tuple-element.605, f32[1024]{0:T(1024)S(1)} %bitcast.115, bf16[511,1024]{1,0:T(8,128)(2,1)S(1)} %get-tuple-element.679, s32[]{:T(128)S(6)} %select_n.1373, f32[1024]{0:T(1024)S(1)} %bitcast.116, s32[]{:T(128)S(6)} %select_n.1374, ...), kind=kLoop, calls=%fused_computation.26.clone.1 | loop fusion | flops 33816576 | bytes 19013760 | tf_op jit(solution)/shard_map/while/body/eval_jaxpr/add | solution.py:65
  197.3 1.3 constant_dynamic-slice_fusion.35
  198.7 1.5 constant_dynamic-slice_fusion.34
  200.5 12.2 %select_add_fusion.3 = f32[256,1024]{1,0:T(8,128)S(1)} fusion(f32[256,1024]{1,0:T(8,128)S(1)} %get-tuple-element.605, f32[1024]{0:T(1024)S(1)} %bitcast.115, bf16[511,1024]{1,0:T(8,128)(2,1)S(1)} %get-tuple-element.679, s32[]{:T(128)S(6)} %select_n.1373, f32[1024]{0:T(1024)S(1)} %bitcast.116, s32[]{:T(128)S(6)} %select_n.1374, ...), kind=kLoop, calls=%fused_computation.26.clone.1 | loop fusion | flops 33816576 | bytes 19013760 | tf_op jit(solution)/shard_map/while/body/eval_jaxpr/add | solution.py:65
  212.8 1.5 constant_dynamic-slice_fusion.35
  214.4 1.6 constant_dynamic-slice_fusion.34
  216.4 12.2 %select_add_fusion.3 = f32[256,1024]{1,0:T(8,128)S(1)} fusion(f32[256,1024]{1,0:T(8,128)S(1)} %get-tuple-element.605, f32[1024]{0:T(1024)S(1)} %bitcast.115, bf16[511,1024]{1,0:T(8,128)(2,1)S(1)} %get-tuple-element.679, s32[]{:T(128)S(6)} %select_n.1373, f32[1024]{0:T(1024)S(1)} %bitcast.116, s32[]{:T(128)S(6)} %select_n.1374, ...), kind=kLoop, calls=%fused_computation.26.clone.1 | loop fusion | flops 33816576 | bytes 19013760 | tf_op jit(solution)/shard_map/while/body/eval_jaxpr/add | solution.py:65
  228.6 0.2 fusion.51
  228.8 0.0 copy-start.1
  228.8 1.3 copy-done.1
  230.2 0.3 multiply_reduce_fusion.1
  230.4 0.0 all-gather.5.cloned.1.call-done
  230.5 3.9 %fusion.26 = f32[256,1024]{1,0:T(8,128)} fusion(bf16[1024,2048]{1,0:T(8,128)(2,1)} %all-gather.5.cloned.1.call-done, f32[1024]{0:T(1024)S(1)} %bitcast.153, f32[256]{0:T(256)S(1)} %add_rsqrt_fusion.1, f32[256,1024]{1,0:T(8,128)S(1)} %get-tuple-element.276, f32[511,1024]{1,0:T(8,128)} %copy-done.1), kind=kOutput, calls=%fused_computation.93 | convolution fusion | flops 537919488 | bytes 5248000 | tf_op jit(solution)/shard_map/dot_general | solution.py:76
  234.4 4.8 %fusion.39 = bf16[256,1024]{1,0:T(8,128)(2,1)} fusion(bf16[1,1024,1024]{2,1,0:T(8,128)(2,1)} %all-gather.7.cloned.1.call-done, bf16[1024,2048]{1,0:T(8,128)(2,1)} %all-gather.5.cloned.1.call-done, f32[256,1024]{1,0:T(8,128)} %fusion.26, f32[1024]{0:T(1024)S(1)} %bitcast.154, f32[256]{0:T(256)S(1)} %add_rsqrt_fusion.1, ...), kind=kOutput, calls=%fused_computation.102 | convolution fusion | flops 1077149696 | bytes 9966592 | tf_op jit(solution)/shard_map/dot_general | solution.py:80
  (33 shorter events, 0.6 us)
Async XLA Ops:
  6.5 223.9 %all-gather.5.cloned.1.call-start = ((), (), s32[]{:S(2)}) async-start(), calls=%async_computation.1 | async-start | bytes 4325376 | tf_op jit(solution)/shard_map/all_gather | solution.py:21
  11.2 23.2 %copy-start.7 = (s32[256]{0:T(256)S(1)}, s32[256]{0:T(256)}, u32[]{:S(2)}) copy-start(s32[256]{0:T(256)} %param.11) | copy-start | bytes 3076
  11.2 28.8 %copy-start.4 = (bf16[1,32,1024]{2,1,0:T(8,128)(2,1)S(1)}, bf16[1,32,1024]{2,1,0:T(8,128)(2,1)}, u32[]{:S(2)}) copy-start(bf16[1,32,1024]{2,1,0:T(8,128)(2,1)} %param.19) | copy-start | bytes 196612
  11.2 81.0 %copy-start.8 = (s32[32]{0:T(128)S(1)}, s32[32]{0:T(128)}, u32[]{:S(2)}) copy-start(s32[32]{0:T(128)} %param.12) | copy-start | bytes 388
  11.2 81.4 %copy-start.5 = (f32[1,2,1024]{2,1,0:T(2,128)S(1)}, f32[1,2,1024]{2,1,0:T(2,128)}, u32[]{:S(2)}) copy-start(f32[1,2,1024]{2,1,0:T(2,128)} %param.16) | copy-start | bytes 24580
  11.2 81.4 %copy-start.3 = (bf16[1,256,1024]{2,1,0:T(8,128)(2,1)S(1)}, bf16[1,256,1024]{2,1,0:T(8,128)(2,1)}, u32[]{:S(2)}) copy-start(bf16[1,256,1024]{2,1,0:T(8,128)(2,1)} %param.15) | copy-start | bytes 1572868
  11.2 81.4 %copy-start.6 = (s32[1,1024]{1,0:T(1,128)S(1)}, s32[1,1024]{1,0:T(1,128)}, u32[]{:S(2)}) copy-start(s32[1,1024]{1,0:T(1,128)} %param.14) | copy-start | bytes 12292
  11.3 82.8 %all-to-all-start = ((bf16[512,2,1024]{2,1,0:T(2,128)(2,1)}), bf16[512,2,1024]{2,1,0:T(2,128)(2,1)}, u32[]{:S(2)}, u32[]{:S(2)}) async-start(bf16[512,2,1024]{2,1,0:T(2,128)(2,1)} %stack.2), calls=%async_computation | async-start | bytes 4194304 | tf_op jit(solution)/shard_map/all_to_all | solution.py:99
  34.4 200.1 %all-gather.7.cloned.1.call-start = ((), (), s32[]{:S(2)}) async-start(), calls=%async_computation.2 | async-start | bytes 2359296 | tf_op jit(solution)/shard_map/all_gather | solution.py:31
  34.4 59.5 %collective-permute-start = (s32[256]{0:T(256)S(1)}, s32[256]{0:T(256)S(1)}, u32[]{:S(2)}, u32[]{:S(2)}) collective-permute-start(s32[256]{0:T(256)S(1)} %copy-done.7), channel_id=1, source_target_pairs={{0,1},{1,2},{2,3},{3,4},{4,5},{5,6},{6,7},{7,8},{8,9},{9,10},{10,1... | collective-permute-start | bytes 3080 | tf_op jit(solution)/shard_map/ppermute | solution.py:16
  102.9 125.7 %copy-start = (bf16[511,1024]{1,0:T(8,128)(2,1)S(1)}, bf16[511,1024]{1,0:T(8,128)(2,1)}, u32[]{:S(2)}) copy-start(bf16[511,1024]{1,0:T(8,128)(2,1)} %gather_fusion) | copy-start | bytes 3139588
  228.8 1.3 copy-start.1
  230.5 3.9 %copy-start.2 = (f32[511,1024]{1,0:T(8,128)S(1)}, f32[511,1024]{1,0:T(8,128)}, u32[]{:S(2)}) copy-start(f32[511,1024]{1,0:T(8,128)} %copy-done.1) | copy-start | bytes 6279172
Sparse Core Ops, SparseCore 0:
  10.5 134.5 all-gather.4
  147.2 41.5 all-gather.6
